TPU v7x, 32 devices: a whole 2x2x4 slice. The times are simulated.
32 devices in a mesh: farcp: 4 (over x, core), nearcp: 4 (over z), heads: 2 (over y).
Axes of the slice: x: 2, y: 2, z: 4, core: 2. Of those that a mesh axis runs over, the one named last changes fastest.
Arguments:
- raw_keys: bfloat16 [16, 24576, 8, 128], P(None, ('farcp', 'nearcp'), 'heads'), may hold values from -6 to 6
- raw_values: bfloat16 [16, 24576, 8, 128], P(None, ('farcp', 'nearcp'), 'heads'), may hold values from -6 to 6
- turn_angle: float32 [24576, 64], replicated, may hold values from -3.140625 to 3.140625
Outputs:
- stored_keys: bfloat16 [16, 8, 128, 24576], P(('farcp', 'nearcp'), 'heads')
- stored_values: bfloat16 [16, 24576, 8, 128], P(('farcp', 'nearcp'), None, 'heads')
- page_high: bfloat16 [16, 384, 8, 128], P(('farcp', 'nearcp'), None, 'heads')
- page_low: bfloat16 [16, 384, 8, 128], P(('farcp', 'nearcp'), None, 'heads')
All inputs are finite; a program needn't handle non-finite values.
Results may differ from a plain program's by a relative error of at most 0.001.
Values may be sent and summed in bfloat16 or wider, within the bound.
No kernel may reach another device: no remote copies, remote signals or barrier semaphores. Data moves between devices by JAX's collectives and lax.ppermute only.
A program may use at most 256 MiB of HBM per device.

v0:
```python
import jax
import jax.numpy as jnp
from jax import lax
from jax.sharding import PartitionSpec as P

PAGE = 64


def apply_rotary(vectors, angle):
    half = vectors.shape[-1] // 2
    cosine, sine = (jnp.cos(angle)[None, :, None, :], jnp.sin(angle)[None, :, None, :])
    first, second = (vectors[..., :half], vectors[..., half:])
    return jnp.concatenate(
        [first * cosine - second * sine, second * cosine + first * sine], axis=-1
    )


def keys_in_place(plain_keys, angle):
    wide_keys = plain_keys.astype(jnp.float32)
    return apply_rotary(wide_keys, angle)


def per_device(raw_keys, raw_values, turn_angle):
    my_angles = lax.dynamic_slice_in_dim(
        turn_angle, lax.axis_index(("farcp", "nearcp")) * raw_keys.shape[1], raw_keys.shape[1]
    )
    sent_keys = keys_in_place(raw_keys, my_angles).astype(jnp.bfloat16)
    moved_keys, stored_values = (
        lax.all_to_all(sent_keys, ("farcp", "nearcp"), split_axis=0, concat_axis=1, tiled=True),
        lax.all_to_all(raw_values, ("farcp", "nearcp"), split_axis=0, concat_axis=1, tiled=True),
    )
    page_view = moved_keys.reshape(
        moved_keys.shape[0], -1, PAGE, moved_keys.shape[2], moved_keys.shape[3]
    )
    page_high = jnp.max(page_view, axis=2)
    page_low = jnp.min(page_view, axis=2)
    stored_keys = jnp.transpose(moved_keys, (0, 2, 3, 1))
    return (stored_keys, stored_values, page_high, page_low)


def solution(mesh):
    return jax.shard_map(
        per_device,
        mesh=mesh,
        in_specs=(
            P(None, ("farcp", "nearcp"), "heads", None),
            P(None, ("farcp", "nearcp"), "heads", None),
            P(),
        ),
        out_specs=(
            P(("farcp", "nearcp"), "heads", None, None),
            P(("farcp", "nearcp"), None, "heads", None),
            P(("farcp", "nearcp"), None, "heads", None),
            P(("farcp", "nearcp"), None, "heads", None),
        ),
        check_vma=False,
    )
```

profile of v0, /device:TPU:4, one launch (start us, length us, event | category | flops | bytes accessed | tf_op | source)
XLA Modules:
  0.0 1232.2 jit_solution(8686672545005040533)
XLA Ops:
  0.6 2.3 dynamic-slice_cosine_fusion
  3.0 0.3 copy.7
  3.2 0.3 copy.8
  3.5 23.9 %convert_element_type.4 = f32[16,1536,4,128]{3,2,1,0:T(4,128)} convert(bf16[16,1536,4,128]{3,2,1,0:T(4,128)(2,1)} %param.3) | non-fusion elementwise | flops 12582912 | bytes 75497472 | tf_op jit(solution)/shard_map/convert_element_type | solution.py:19
  27.5 49.4 %subtract_convert_fusion = (bf16[16,1536,4,64]{3,2,1,0:T(4,128)(2,1)}, bf16[16,1536,4,64]{3,2,1,0:T(4,128)(2,1)}) fusion(f32[16,1536,4,128]{3,2,1,0:T(4,128)} %convert_element_type.4, f32[1536,64]{1,0:T(8,128)S(1)} %copy.8, f32[1536,64]{1,0:T(8,128)S(1)} %copy.7), kind=kLoop, calls=%fused_computation.1 | loop fusion | flops 50331648 | bytes 76283904 | tf_op jit(solution)/shard_map/convert
  76.9 37.5 %pad_maximum_fusion = bf16[16,1536,4,128]{3,2,1,0:T(4,128)(2,1)} fusion(bf16[16,1536,4,64]{3,2,1,0:T(4,128)(2,1)} %get-tuple-element.7, bf16[16,1536,4,64]{3,2,1,0:T(4,128)(2,1)} %get-tuple-element.6), kind=kLoop, calls=%fused_computation.2 | loop fusion | flops 50331648 | bytes 50331648 | tf_op jit(solution)/shard_map/concatenate | solution.py:13
  114.4 551.3 %all_to_all.24 = bf16[16,1536,4,128]{3,2,1,0:T(4,128)(2,1)} all-to-all(bf16[16,1536,4,128]{3,2,1,0:T(4,128)(2,1)} %pad_maximum_fusion), channel_id=1, replica_groups=mesh['farcp'=4,'nearcp'=4,'heads'=2] {'farcp','nearcp'}, dimensions={0} | all-to-all | bytes 50331648 | tf_op jit(solution)/shard_map/all_to_all | solution.py:29
  665.7 5.6 all-to-all-start.1
  671.3 38.5 %copy.10 = bf16[1,24576,4,128]{1,3,2,0:T(8,128)(2,1)} copy(bf16[1,24576,4,128]{3,2,1,0:T(4,128)(2,1)} %bitcast.6) | data formatting | bytes 50331648 | tf_op jit(solution)/shard_map/all_to_all | solution.py:29
  709.8 19.2 %fusion = (bf16[384,4,128]{2,1,0:T(4,128)(2,1)}, bf16[384,4,128]{2,1,0:T(4,128)(2,1)}) fusion(bf16[1,384,64,4,128]{4,3,2,1,0:T(4,128)(2,1)} %bitcast.7), kind=kLoop, calls=%fused_computation.5 | loop fusion | flops 24772608 | bytes 25952256 | tf_op jit(solution)/shard_map/reduce_min | solution.py:36
  729.0 486.0 %all-to-all-done.1 = bf16[16,1536,4,128]{3,2,1,0:T(4,128)(2,1)} async-done(((bf16[16,1536,4,128]{3,2,1,0:T(4,128)(2,1)}), bf16[16,1536,4,128]{3,2,1,0:T(4,128)(2,1)}, u32[]{:S(2)}, u32[]{:S(2)}) %all-to-all-start.1) | async-done | bytes 25165856 | tf_op jit(solution)/shard_map/all_to_all | solution.py:30
  1215.0 17.2 %copy.12 = bf16[1,24576,4,128]{3,2,1,0:T(4,128)(2,1)} copy(bf16[1,24576,4,128]{3,2,1,0:T(4,128)(2,1)} %bitcast.2) | data formatting | bytes 50331648
Async XLA Ops:
  665.7 549.3 %all-to-all-start.1 = ((bf16[16,1536,4,128]{3,2,1,0:T(4,128)(2,1)}), bf16[16,1536,4,128]{3,2,1,0:T(4,128)(2,1)}, u32[]{:S(2)}, u32[]{:S(2)}) async-start(bf16[16,1536,4,128]{3,2,1,0:T(4,128)(2,1)} %param.4), calls=%async_computation.1 | async-start | bytes 50331648 | tf_op jit(solution)/shard_map/all_to_all | solution.py:30
where the time goes:
time: 1230 us
  blocking collectives  551 us (45%)
  waiting for transfers between devices  486 us (40%)
  other arithmetic  130 us (11%)
  local copies, waits for them, and re-layouts  58.5 us (5%)
    all_to_all x1, blocking collectives, per_device(): lax.all_to_all(sent_keys, ('farcp', 'nearcp'), split_axis=0, concat_axis=...  551 us
    all_to_all x1, waiting for transfers between devices, per_device(): lax.all_to_all(raw_values, ('farcp', 'nearcp'), split_axis=0, concat_axis...  486 us
    another operation x1, other arithmetic  49.4 us
    all_to_all x1, local copies, waits for them, and re-layouts, per_device(): lax.all_to_all(sent_keys, ('farcp', 'nearcp'), split_axis=0, concat_axis=...  38.5 us
    concatenate x1, other arithmetic, apply_rotary(): jnp.concatenate([first * cosine - second * sine, second * cosine + first...  37.5 us
  transfers between devices with their start and end apart: 1, of which 1 were waited for; matrix products, arithmetic and copies ran while one was open for 5% of the time, Pallas kernels for 0%

commit v1 on v0

--- a/solution.py
+++ b/solution.py
@@ -4,6 +4,8 @@
 from jax.sharding import PartitionSpec as P
 
 PAGE = 64
+GROUP = ("farcp", "nearcp")
+SHARES = (4, 11, 1)
 
 
 def apply_rotary(vectors, angle):
@@ -15,20 +17,38 @@
     )
 
 
-def keys_in_place(plain_keys, angle):
-    wide_keys = plain_keys.astype(jnp.float32)
-    return apply_rotary(wide_keys, angle)
+def exchange(block):
+    return lax.all_to_all(block, GROUP, split_axis=0, concat_axis=0, tiled=True)
 
 
 def per_device(raw_keys, raw_values, turn_angle):
+    length = raw_keys.shape[1]
+    cuts = [0]
+    for share in SHARES:
+        cuts.append(cuts[-1] + length * share // sum(SHARES))
+    parts = [raw_values[:, a:b] for a, b in zip(cuts, cuts[1:])]
+
+    head_in, keys_in = lax.optimization_barrier((parts[0], raw_keys))
+    head = exchange(head_in)
+
     my_angles = lax.dynamic_slice_in_dim(
-        turn_angle, lax.axis_index(("farcp", "nearcp")) * raw_keys.shape[1], raw_keys.shape[1]
+        turn_angle, lax.axis_index(GROUP) * length, length
     )
-    sent_keys = keys_in_place(raw_keys, my_angles).astype(jnp.bfloat16)
-    moved_keys, stored_values = (
-        lax.all_to_all(sent_keys, ("farcp", "nearcp"), split_axis=0, concat_axis=1, tiled=True),
-        lax.all_to_all(raw_values, ("farcp", "nearcp"), split_axis=0, concat_axis=1, tiled=True),
-    )
+    sent_keys = apply_rotary(keys_in.astype(jnp.float32), my_angles).astype(jnp.bfloat16)
+    sent_keys, head = lax.optimization_barrier((sent_keys, head))
+    moved_keys = exchange(sent_keys)
+
+    body_in, moved_keys = lax.optimization_barrier((parts[1], moved_keys))
+    body = exchange(body_in)
+    tail_in, body = lax.optimization_barrier((parts[2], body))
+    tail = exchange(tail_in)
+
+    stored_values = jnp.zeros(raw_values.shape, raw_values.dtype)
+    for start, part in zip(cuts, (head, body, tail)):
+        stored_values = lax.dynamic_update_slice_in_dim(stored_values, part, start, 1)
+    stored_values = stored_values.reshape((1, -1) + raw_values.shape[2:])
+
+    moved_keys = moved_keys.reshape((1, -1) + raw_keys.shape[2:])
     page_view = moved_keys.reshape(
         moved_keys.shape[0], -1, PAGE, moved_keys.shape[2], moved_keys.shape[3]
     )

time: 1230 us -> 1130 us (0.919)
  blocking collectives: 551 us -> 0 us
  waiting for transfers between devices: 486 us -> 880 us
  local copies, waits for them, and re-layouts: 58.5 us -> 95.3 us
  starting transfers between devices: 5.61 us -> 20.4 us
    all_to_all x1 -> x0, blocking collectives: 551 us -> none  [per_device(): lax.all_to_all(sent_keys, ('farcp', 'nearcp'), split_axis=0, concat_axis=...]
    all_to_all x1 -> x4, waiting for transfers between devices: 486 us -> 880 us  [exchange(): return lax.all_to_all(block, GROUP, split_axis=0, concat_axis=0, tiled=True)]
    all_to_all x1 -> x0, local copies, waits for them, and re-layouts: 38.5 us -> none  [per_device(): lax.all_to_all(sent_keys, ('farcp', 'nearcp'), split_axis=0, concat_axis=...]
    reshape x0 -> x1, local copies, waits for them, and re-layouts: none -> 38.5 us  [per_device(): moved_keys = moved_keys.reshape((1, -1) + raw_keys.shape[2:])]
    dynamic_update_slice x0 -> x3, local copies, waits for them, and re-layouts: none -> 30.8 us  [per_device(): lax.dynamic_update_slice_in_dim(stored_values, part, start, 1)]
    slice x0 -> x3, local copies, waits for them, and re-layouts: none -> 23.2 us  [per_device(): parts = [raw_values[:, a:b] for a, b in zip(cuts, cuts[1:])]]
    unnamed x1 -> x0, local copies, waits for them, and re-layouts: 17.2 us -> none
    all_to_all x1 -> x4, starting transfers between devices: 5.61 us -> 20.4 us  [exchange(): return lax.all_to_all(block, GROUP, split_axis=0, concat_axis=0, tiled=True)]
  transfers between devices with their start and end apart: 1 -> 4, of which waited for: 1 -> 4; matrix products, arithmetic and copies ran while one was open for 5% -> 19% of each run, Pallas kernels for 0% -> 0%
where the time goes in v1:
time: 1130 us
  waiting for transfers between devices  880 us (78%)
  other arithmetic  130 us (12%)
  local copies, waits for them, and re-layouts  95.3 us (8%)
  starting transfers between devices  20.4 us (2%)
    all_to_all x4, waiting for transfers between devices, exchange(): return lax.all_to_all(block, GROUP, split_axis=0, concat_axis=0, tiled=True)  880 us
    another operation x1, other arithmetic  49.4 us
    reshape x1, local copies, waits for them, and re-layouts, per_device(): moved_keys = moved_keys.reshape((1, -1) + raw_keys.shape[2:])  38.5 us
    concatenate x1, other arithmetic, apply_rotary(): jnp.concatenate([first * cosine - second * sine, second * cosine + first...  37.5 us
    dynamic_update_slice x3, local copies, waits for them, and re-layouts, per_device(): lax.dynamic_update_slice_in_dim(stored_values, part, start, 1)  30.8 us
    convert_element_type x1, other arithmetic, per_device(): keys_in.astype(jnp.float32)  23.9 us
    slice x3, local copies, waits for them, and re-layouts, per_device(): parts = [raw_values[:, a:b] for a, b in zip(cuts, cuts[1:])]  23.2 us
  transfers between devices with their start and end apart: 4, of which 4 were waited for; matrix products, arithmetic and copies ran while one was open for 19% of the time, Pallas kernels for 0%

profile of v1, /device:TPU:4, one launch (start us, length us, event | category | flops | bytes accessed | tf_op | source)
XLA Modules:
  0.0 1126.7 jit_solution(9005219652091450751)
XLA Ops:
  0.6 7.7 slice.16
  8.3 6.0 all-to-all-start
  14.3 2.3 dynamic-slice_cosine_fusion
  16.6 0.3 copy.7
  16.9 0.3 copy.8
  17.2 23.9 %convert_element_type.4 = f32[16,1536,4,128]{3,2,1,0:T(4,128)} convert(bf16[16,1536,4,128]{3,2,1,0:T(4,128)(2,1)} %param.3) | non-fusion elementwise | flops 12582912 | bytes 75497472 | tf_op jit(solution)/shard_map/convert_element_type | solution.py:37
  41.1 49.4 %subtract_convert_fusion = (bf16[16,1536,4,64]{3,2,1,0:T(4,128)(2,1)}, bf16[16,1536,4,64]{3,2,1,0:T(4,128)(2,1)}) fusion(f32[16,1536,4,128]{3,2,1,0:T(4,128)} %convert_element_type.4, f32[1536,64]{1,0:T(8,128)S(1)} %copy.8, f32[1536,64]{1,0:T(8,128)S(1)} %copy.7), kind=kLoop, calls=%fused_computation.1 | loop fusion | flops 50331648 | bytes 76283904 | tf_op jit(solution)/shard_map/convert
  90.5 37.5 %pad_maximum_fusion = bf16[16,1536,4,128]{3,2,1,0:T(4,128)(2,1)} fusion(bf16[16,1536,4,64]{3,2,1,0:T(4,128)(2,1)} %get-tuple-element.23, bf16[16,1536,4,64]{3,2,1,0:T(4,128)(2,1)} %get-tuple-element.22), kind=kLoop, calls=%fused_computation.2 | loop fusion | flops 50331648 | bytes 50331648 | tf_op jit(solution)/shard_map/concatenate | solution.py:15
  128.0 25.5 %all-to-all-done = bf16[16,384,4,128]{3,2,1,0:T(4,128)(2,1)} async-done(((bf16[16,384,4,128]{3,2,1,0:T(4,128)(2,1)}), bf16[16,384,4,128]{3,2,1,0:T(4,128)(2,1)}, u32[]{:S(2)}, u32[]{:S(2)}) %all-to-all-start) | async-done | bytes 6291488 | tf_op jit(solution)/shard_map/all_to_all | solution.py:21
  153.5 5.5 all-to-all-start.1
  159.1 12.3 %slice.15 = bf16[16,1056,4,128]{3,2,1,0:T(4,128)(2,1)} slice(bf16[16,1536,4,128]{3,2,1,0:T(4,128)(2,1)} %param.4), slice={[0:16], [384:1440], [0:4], [0:128]} | slice | bytes 34603008 | tf_op jit(solution)/shard_map/slice | solution.py:29
  171.4 531.4 %all-to-all-done.1 = bf16[16,1536,4,128]{3,2,1,0:T(4,128)(2,1)} async-done(((bf16[16,1536,4,128]{3,2,1,0:T(4,128)(2,1)}), bf16[16,1536,4,128]{3,2,1,0:T(4,128)(2,1)}, u32[]{:S(2)}, u32[]{:S(2)}) %all-to-all-start.1) | async-done | bytes 25165856 | tf_op jit(solution)/shard_map/all_to_all | solution.py:21
  702.8 5.2 all-to-all-start.2
  708.0 3.2 slice.19
  711.2 16.8 %dynamic_update_slice.9 = bf16[16,1536,4,128]{3,2,1,0:T(4,128)(2,1)} pad(bf16[16,384,4,128]{3,2,1,0:T(4,128)(2,1)} %all-to-all-done, bf16[]{:T(256)} %constant.9.clone.1), padding=0_0x0_1152x0_0x0_0 | pad | bytes 31457282 | tf_op jit(solution)/shard_map/dynamic_update_slice | solution.py:48
  728.0 38.5 %copy.10 = bf16[1,24576,4,128]{1,3,2,0:T(8,128)(2,1)} copy(bf16[1,24576,4,128]{3,2,1,0:T(4,128)(2,1)} %bitcast) | data formatting | bytes 50331648 | tf_op jit(solution)/shard_map/reshape | solution.py:51
  766.5 316.7 %all-to-all-done.2 = bf16[16,1056,4,128]{3,2,1,0:T(4,128)(2,1)} async-done(((bf16[16,1056,4,128]{3,2,1,0:T(4,128)(2,1)}), bf16[16,1056,4,128]{3,2,1,0:T(4,128)(2,1)}, u32[]{:S(2)}, u32[]{:S(2)}) %all-to-all-start.2) | async-done | bytes 17301536 | tf_op jit(solution)/shard_map/all_to_all | solution.py:21
  1083.2 3.7 all-to-all-start.3
  1086.9 19.2 %fusion = (bf16[384,4,128]{2,1,0:T(4,128)(2,1)}, bf16[384,4,128]{2,1,0:T(4,128)(2,1)}) fusion(bf16[1,384,64,4,128]{4,3,2,1,0:T(4,128)(2,1)} %bitcast.3), kind=kLoop, calls=%fused_computation.7 | loop fusion | flops 24772608 | bytes 25952256 | tf_op jit(solution)/shard_map/reduce_min | solution.py:56
  1106.1 12.3 %constant_dynamic-update-slice_fusion.1 = bf16[16,1536,4,128]{3,2,1,0:T(4,128)(2,1)} fusion(bf16[16,1536,4,128]{3,2,1,0:T(4,128)(2,1)} %dynamic_update_slice.9, bf16[16,1056,4,128]{3,2,1,0:T(4,128)(2,1)} %all-to-all-done.2), kind=kLoop, calls=%fused_computation.6 | loop fusion | bytes 34603008 | tf_op jit(solution)/shard_map/dynamic_update_slice | solution.py:48
  1118.4 6.6 all-to-all-done.3
  1125.0 1.7 constant_dynamic-update-slice_fusion
Async XLA Ops:
  8.3 145.2 %all-to-all-start = ((bf16[16,384,4,128]{3,2,1,0:T(4,128)(2,1)}), bf16[16,384,4,128]{3,2,1,0:T(4,128)(2,1)}, u32[]{:S(2)}, u32[]{:S(2)}) async-start(bf16[16,384,4,128]{3,2,1,0:T(4,128)(2,1)} %slice.16), calls=%async_computation | async-start | bytes 12582912 | tf_op jit(solution)/shard_map/all_to_all | solution.py:21
  153.5 549.2 %all-to-all-start.1 = ((bf16[16,1536,4,128]{3,2,1,0:T(4,128)(2,1)}), bf16[16,1536,4,128]{3,2,1,0:T(4,128)(2,1)}, u32[]{:S(2)}, u32[]{:S(2)}) async-start(bf16[16,1536,4,128]{3,2,1,0:T(4,128)(2,1)} %pad_maximum_fusion), calls=%async_computation.1 | async-start | bytes 50331648 | tf_op jit(solution)/shard_map/all_to_all | solution.py:21
  702.8 380.4 %all-to-all-start.2 = ((bf16[16,1056,4,128]{3,2,1,0:T(4,128)(2,1)}), bf16[16,1056,4,128]{3,2,1,0:T(4,128)(2,1)}, u32[]{:S(2)}, u32[]{:S(2)}) async-start(bf16[16,1056,4,128]{3,2,1,0:T(4,128)(2,1)} %slice.15), calls=%async_computation.2 | async-start | bytes 34603008 | tf_op jit(solution)/shard_map/all_to_all | solution.py:21
  1083.2 41.8 %all-to-all-start.3 = ((bf16[16,96,4,128]{3,2,1,0:T(4,128)(2,1)}), bf16[16,96,4,128]{3,2,1,0:T(4,128)(2,1)S(1)}, u32[]{:S(2)}, u32[]{:S(2)}) async-start(bf16[16,96,4,128]{3,2,1,0:T(4,128)(2,1)} %slice.19), calls=%async_computation.3 | async-start | bytes 3145728 | tf_op jit(solution)/shard_map/all_to_all | solution.py:21
